TPU v7x, 32 devices: a whole 2x2x4 slice. The times are simulated.
32 devices in a mesh: gx: 4 (over y, core), gy: 8 (over z, x).
Axes of the slice: x: 2, y: 2, z: 4, core: 2. Of those that a mesh axis runs over, the one named last changes fastest.
Arguments:
- hidden_states: bfloat16 [1024, 128], replicated, may hold values from -60 to 60
- item_table: bfloat16 [262144, 128], P(('gx', 'gy')), may hold values from -1.796875 to 1.796875
- targets: int32 [1024], replicated, may hold values from 0 to 262143
Outputs:
- expected: float32 [1024, 128], P(('gx', 'gy'))
- nll: float32 [1024], P(('gx', 'gy'))
All inputs are finite; a program needn't handle non-finite values.
Results may differ from a plain program's by a relative error of at most 0.0023.
Values sent between devices are 32-bit elements; how exact they have to be, the bound alone decides.
No kernel may reach another device: no remote copies, remote signals or barrier semaphores. Data moves between devices by JAX's collectives and lax.ppermute only.
A program may use at most 64 MiB of HBM per device.

v0:
```python
import jax
import jax.numpy as jnp
from jax import lax
from jax.sharding import PartitionSpec as P

BLK = 512


def local(hidden_states, item_table, targets):
    positions = hidden_states.shape[0]
    shard_items = item_table.shape[0]
    nblocks = shard_items // BLK

    def visit_block(block_index, carry):
        highest, totals, weighted = carry
        block = lax.dynamic_slice_in_dim(item_table, block_index * BLK, BLK, 0)
        scores = lax.dot_general(
            hidden_states, block, (((1,), (1,)), ((), ())), preferred_element_type=jnp.float32
        )
        block_max = jnp.max(scores, axis=1)
        exponent = jnp.exp(scores - block_max[:, None])
        block_sum = jnp.sum(exponent, axis=1)
        probs_low = exponent.astype(jnp.bfloat16)
        block_acc = jnp.dot(probs_low, block, preferred_element_type=jnp.float32)
        new_max = jnp.maximum(highest, block_max)
        retain = jnp.exp(highest - new_max)
        rescale = jnp.exp(block_max - new_max)
        totals = totals * retain + block_sum * rescale
        weighted = weighted * retain[:, None] + block_acc * rescale[:, None]
        return (new_max, totals, weighted)

    start_state = (
        jnp.full((positions,), -1e30, jnp.float32),
        jnp.zeros((positions,), jnp.float32),
        jnp.zeros((positions, item_table.shape[1]), jnp.float32),
    )
    highest, totals, weighted = lax.fori_loop(0, nblocks, visit_block, start_state)
    device_index = lax.axis_index(("gx", "gy"))
    local_index = targets - device_index * shard_items
    owner_mask = (local_index >= 0) & (local_index < shard_items)
    target_rows = item_table[jnp.clip(local_index, 0, shard_items - 1)]
    own_logit = jnp.sum(hidden_states.astype(jnp.float32) * target_rows.astype(jnp.float32), axis=1)
    own_logit = jnp.where(owner_mask, own_logit, 0.0)
    row_count = positions // lax.axis_size(("gx", "gy"))
    first_row = device_index * row_count
    global_max = lax.pmax(highest, ("gx", "gy"))
    factor = jnp.exp(highest - global_max)
    weighted_rows, total_rows, target_part = (
        lax.psum_scatter(weighted * factor[:, None], ("gx", "gy"), scatter_dimension=0, tiled=True),
        lax.psum_scatter(totals * factor, ("gx", "gy"), scatter_dimension=0, tiled=True),
        lax.psum_scatter(own_logit, ("gx", "gy"), scatter_dimension=0, tiled=True),
    )
    max_rows = lax.dynamic_slice_in_dim(global_max, first_row, row_count, 0)
    expected = weighted_rows / total_rows[:, None]
    nll = max_rows + jnp.log(total_rows) - target_part
    return (expected, nll)


def solution(mesh):
    return jax.shard_map(
        local,
        mesh=mesh,
        in_specs=(P(), P(("gx", "gy"), None), P()),
        out_specs=(P(("gx", "gy"), None), P(("gx", "gy"))),
        check_vma=False,
    )
```

profile of v0, /device:TPU:0, one launch (start us, length us, event | category | flops | bytes accessed | tf_op | source)
XLA Modules:
  0.0 252.0 jit_solution(11066201469598881349)
XLA Ops:
  7.2 57.6 %while.18 = (s32[]{:T(128)}, f32[1024]{0:T(1024)S(1)}, f32[1024]{0:T(1024)S(1)}, f32[1024,128]{1,0:T(8,128)S(1)}, bf16[8192,128]{1,0:T(8,128)(2,1)}, /*index=5*/...) while((s32[]{:T(128)}, f32[1024]{0:T(1024)S(1)}, f32[1024]{0:T(1024)S(1)}, ...), condition=%wide.region_3.0_spmd.clone, body=%wide.region_0.0_spmd.clone.sunk | while | flops 271587328 | bytes 7921838 | solution.py:37
  7.3 1.5 fusion.25
  8.7 0.3 fusion.26
  9.1 1.8 fusion.28
  10.9 1.5 fusion.25
  12.3 0.3 fusion.26
  12.7 1.8 fusion.28
  14.5 1.5 fusion.25
  16.3 1.8 fusion.28
  18.1 1.5 fusion.25
  19.5 0.3 fusion.26
  19.9 1.8 fusion.28
  21.7 1.5 fusion.25
  23.1 0.3 fusion.26
  23.5 1.8 fusion.28
  25.3 1.5 fusion.25
  26.7 0.3 fusion.26
  27.1 1.8 fusion.28
  28.9 1.5 fusion.25
  30.7 1.8 fusion.28
  32.5 1.5 fusion.25
  34.3 1.8 fusion.28
  36.1 1.5 fusion.25
  37.9 1.8 fusion.28
  39.7 1.5 fusion.25
  41.1 0.3 fusion.26
  41.5 1.8 fusion.28
  43.3 1.5 fusion.25
  45.1 1.8 fusion.28
  46.9 1.5 fusion.25
  48.3 0.3 fusion.26
  48.7 1.8 fusion.28
  50.5 1.5 fusion.25
  52.3 1.8 fusion.28
  54.0 1.5 fusion.25
  55.9 1.8 fusion.28
  57.6 1.5 fusion.25
  59.5 1.8 fusion.28
  61.2 1.5 fusion.25
  62.7 0.3 fusion.26
  63.1 1.8 fusion.28
  64.8 42.0 %pmax.7 = f32[1024]{0:T(1024)S(1)} all-reduce(f32[1024]{0:T(1024)S(1)} %get-tuple-element.114), channel_id=1, replica_groups=mesh['gx'=4,'gy'=8] {'gx','gy'}, use_global_device_ids=true, to_apply=%region_4.5 | all-reduce | flops 1024 | bytes 8192 | tf_op jit(solution)/shard_map/pmax | solution.py:46
  106.9 1.0 broadcast_multiply_fusion
  107.9 4.7 %gather_fusion = bf16[1024,128]{1,0:T(8,128)(2,1)S(1)} fusion(bf16[8192,128]{1,0:T(8,128)(2,1)} %get-tuple-element.242, s32[1024]{0:T(1024)S(1)} %fusion.11), kind=kCustom, calls=%fused_computation | custom fusion | bytes 528384 | tf_op jit(solution)/shard_map/gather | solution.py:41
  112.9 40.2 %all-reduce.2 = (f32[1024]{0:T(1024)S(1)}, f32[1024]{0:T(1024)S(1)}) all-reduce(f32[1024]{0:T(1024)S(1)} %get-tuple-element.157, f32[1024]{0:T(1024)S(1)} %and_select_fusion), channel_id=3, replica_groups=mesh['gx'=4,'gy'=8] {'gx','gy'}, use_global_device_ids=true, to_apply=%region_6.7.clone | all-reduce | flops 2048 | bytes 16384
  153.1 0.6 dynamic-slice_subtract_fusion
  153.7 90.1 %reduce-scatter.2.cloned.1.call-done = f32[32,128]{1,0:T(8,128)} async-done(((f32[1024,128]{1,0:T(8,128)}), f32[32,128]{1,0:T(8,128)}) %reduce-scatter.2.cloned.1.call-update) | async-done | bytes 16400 | tf_op jit(solution)/shard_map/reduce_scatter | solution.py:49
  243.8 1.4 broadcast_divide_fusion
  (37 shorter events, 3.1 us)
Async XLA Ops:
  7.2 236.6 %reduce-scatter.2.cloned.1.call-start = ((), (), s32[]{:S(2)}) async-start(), calls=%async_computation.1 | async-start | bytes 540672 | tf_op jit(solution)/shard_map/reduce_scatter | solution.py:49
  7.2 100.7 %copy-start.1 = (s32[1024]{0:T(1024)S(1)}, s32[1024]{0:T(1024)}, u32[]{:S(2)}) copy-start(s32[1024]{0:T(1024)} %param.7) | copy-start | bytes 12292
  64.8 47.8 %copy-start = (bf16[1024,128]{1,0:T(8,128)(2,1)S(1)}, bf16[1024,128]{1,0:T(8,128)(2,1)}, u32[]{:S(2)}) copy-start(bf16[1024,128]{1,0:T(8,128)(2,1)} %get-tuple-element.241) | copy-start | bytes 786436
Sparse Core Ops, SparseCore 0:
  108.0 135.7 reduce-scatter.1
where the time goes:
time: 253 us; the launch traced here: 252 us
  waiting for transfers between devices  90.1 us (36%)
  blocking collectives  82.2 us (32%)
  matrix products  51.5 us (20%)
  between operations  14.1 us (6%)
  other arithmetic  8.69 us (3%)
  local copies, waits for them, and re-layouts  4.75 us (2%)
    reduce_scatter x1, waiting for transfers between devices, local(): lax.psum_scatter(weighted * factor[:, None], ('gx', 'gy'), scatter_dimens...  90.1 us
    pmax x1, blocking collectives, local(): global_max = lax.pmax(highest, ('gx', 'gy'))  42 us
    unnamed x1, blocking collectives  40.2 us
    dot_general x16, matrix products, visit_block(): block_acc = jnp.dot(probs_low, block, preferred_element_type=jnp.float32)  28 us
    dot_general x16, matrix products, visit_block(): lax.dot_general(hidden_states, block, (((1,), (1,)), ((), ())), preferred...  23.4 us
    reduce_sum x16, other arithmetic, visit_block(): block_sum = jnp.sum(exponent, axis=1)  5.24 us
  transfers between devices with their start and end apart: 1, of which 1 were waited for; matrix products, arithmetic and copies ran while one was open for 2% of the time, Pallas kernels for 0%

commit v1 on v0

--- a/solution.py
+++ b/solution.py
@@ -41,18 +41,26 @@
     target_rows = item_table[jnp.clip(local_index, 0, shard_items - 1)]
     own_logit = jnp.sum(hidden_states.astype(jnp.float32) * target_rows.astype(jnp.float32), axis=1)
     own_logit = jnp.where(owner_mask, own_logit, 0.0)
-    row_count = positions // lax.axis_size(("gx", "gy"))
-    first_row = device_index * row_count
-    global_max = lax.pmax(highest, ("gx", "gy"))
-    factor = jnp.exp(highest - global_max)
-    weighted_rows, total_rows, target_part = (
-        lax.psum_scatter(weighted * factor[:, None], ("gx", "gy"), scatter_dimension=0, tiled=True),
-        lax.psum_scatter(totals * factor, ("gx", "gy"), scatter_dimension=0, tiled=True),
-        lax.psum_scatter(own_logit, ("gx", "gy"), scatter_dimension=0, tiled=True),
+    devices = lax.axis_size(("gx", "gy"))
+    rows = positions // devices
+    stats = jnp.stack([highest, totals, own_logit]).reshape(3, devices, rows)
+    stats = jnp.transpose(stats, (1, 0, 2)).reshape(devices, 3 * rows)
+    lanes = item_table.shape[1]
+    extra = -(-3 * rows // lanes)
+    stats = jnp.pad(stats, ((0, 0), (0, extra * lanes - 3 * rows)))
+    payload = jnp.concatenate(
+        [weighted.reshape(devices, rows, lanes), stats.reshape(devices, extra, lanes)], axis=1
     )
-    max_rows = lax.dynamic_slice_in_dim(global_max, first_row, row_count, 0)
+    got = lax.all_to_all(payload, ("gx", "gy"), 0, 0, tiled=True)
+    parts = got[:, rows:].reshape(devices, extra * lanes)
+    part_max = parts[:, :rows]
+    max_rows = jnp.max(part_max, axis=0)
+    factor = jnp.exp(part_max - max_rows[None])
+    total_rows = jnp.sum(parts[:, rows:2 * rows] * factor, axis=0)
+    target_rows = jnp.sum(parts[:, 2 * rows:3 * rows], axis=0)
+    weighted_rows = jnp.sum(got[:, :rows] * factor[:, :, None], axis=0)
     expected = weighted_rows / total_rows[:, None]
-    nll = max_rows + jnp.log(total_rows) - target_part
+    nll = max_rows + jnp.log(total_rows) - target_rows
     return (expected, nll)
 
 

time: 253 us -> 91.3 us (0.36)
  waiting for transfers between devices: 90.1 us -> 0 us
  blocking collectives: 82.2 us -> 26.2 us
  between operations: 14.1 us -> 0.75 us
    reduce_scatter x1 -> x0, waiting for transfers between devices: 90.1 us -> none  [local(): lax.psum_scatter(weighted * factor[:, None], ('gx', 'gy'), scatter_dimens...]
    pmax x1 -> x0, blocking collectives: 42 us -> none  [local(): global_max = lax.pmax(highest, ('gx', 'gy'))]
    unnamed x1 -> x0, blocking collectives: 40.2 us -> none
    all_to_all x0 -> x1, blocking collectives: none -> 26.2 us  [local(): got = lax.all_to_all(payload, ('gx', 'gy'), 0, 0, tiled=True)]
  transfers between devices with their start and end apart: 1 -> 0, of which waited for: 1 -> 0; matrix products, arithmetic and copies ran while one was open for 2% -> 0% of each run, Pallas kernels for 0% -> 0%
where the time goes in v1:
time: 91.3 us; the launch traced here: 90.6 us
  matrix products  49.7 us (54%)
  blocking collectives  26.2 us (29%)
  other arithmetic  8.2 us (9%)
  local copies, waits for them, and re-layouts  5.12 us (6%)
    dot_general x16, matrix products, visit_block(): block_acc = jnp.dot(probs_low, block, preferred_element_type=jnp.float32)  28.1 us
    all_to_all x1, blocking collectives, local(): got = lax.all_to_all(payload, ('gx', 'gy'), 0, 0, tiled=True)  26.2 us
    dot_general x16, matrix products, visit_block(): lax.dot_general(hidden_states, block, (((1,), (1,)), ((), ())), preferred...  21.6 us
    reduce_sum x16, other arithmetic, visit_block(): block_sum = jnp.sum(exponent, axis=1)  5.39 us
    gather x1, local copies, waits for them, and re-layouts, local(): target_rows = item_table[jnp.clip(local_index, 0, shard_items - 1)]  4.74 us

profile of v1, /device:TPU:0, one launch (start us, length us, event | category | flops | bytes accessed | tf_op | source)
XLA Modules:
  0.0 90.6 jit_solution(12705121168119225774)
XLA Ops:
  0.7 0.7 fusion.13
  1.4 4.7 %gather_fusion = bf16[1024,128]{1,0:T(8,128)(2,1)S(1)} fusion(bf16[8192,128]{1,0:T(8,128)(2,1)} %param.6, s32[1024]{0:T(1024)S(1)} %fusion.13), kind=kCustom, calls=%fused_computation | custom fusion | bytes 528384 | tf_op jit(solution)/shard_map/gather | solution.py:41
  6.5 55.9 %while.18 = (s32[]{:T(128)}, f32[1024]{0:T(1024)S(1)}, f32[1024]{0:T(1024)S(1)}, f32[1024,128]{1,0:T(8,128)S(1)}, bf16[8192,128]{1,0:T(8,128)(2,1)}, /*index=5*/...) while((s32[]{:T(128)}, f32[1024]{0:T(1024)S(1)}, ...), condition=%wide.region_3.0_spmd.clone, body=%wide.region_0.0_spmd.clone.sunk | while | flops 271587328 | bytes 7921838 | solution.py:37
  6.5 1.3 %fusion.26 = (f32[1024]{0:T(1024)S(1)}, f32[512,1024]{1,0:T(8,128)S(1)}) fusion(bf16[1024,128]{1,0:T(8,128)(2,1)S(1)} %get-tuple-element.232, bf16[8192,128]{1,0:T(8,128)(2,1)} %get-tuple-element.231, s32[]{:T(128)S(6)} %select_n.22), kind=kOutput, calls=%fused_computation.33.clone.1 | convolution fusion | flops 134740992 | bytes 2494468 | tf_op jit(solution)/shard_map/while/body/eval_jaxpr/dot_general | solution.py:17
  7.9 0.3 fusion.27
  8.2 1.8 %fusion.29 = f32[1024,128]{1,0:T(8,128)S(1)} fusion(f32[512,1024]{1,0:T(8,128)S(1)} %get-tuple-element.201, f32[1024]{0:T(1024)S(1)} %get-tuple-element.202, f32[1024,128]{1,0:T(8,128)S(1)} %get-tuple-element.220, f32[1024]{0:T(1024)S(1)} %get-tuple-element.205, f32[1024]{0:T(1024)S(1)} %get-tuple-element.206, pred[]{:T(512)S(6)} %compare.4, ...), kind=kOutput, calls=%fused_computation.5.clone.1 | convolution fusion | flops 135790592 | bytes 3289093 | tf_op jit(solution)/shard_map/while/body/eval_jaxpr/dot_general | solution.py:24
  10.0 1.3 %fusion.26 = (f32[1024]{0:T(1024)S(1)}, f32[512,1024]{1,0:T(8,128)S(1)}) fusion(bf16[1024,128]{1,0:T(8,128)(2,1)S(1)} %get-tuple-element.232, bf16[8192,128]{1,0:T(8,128)(2,1)} %get-tuple-element.231, s32[]{:T(128)S(6)} %select_n.22), kind=kOutput, calls=%fused_computation.33.clone.1 | convolution fusion | flops 134740992 | bytes 2494468 | tf_op jit(solution)/shard_map/while/body/eval_jaxpr/dot_general | solution.py:17
  11.4 0.3 fusion.27
  11.7 1.8 %fusion.29 = f32[1024,128]{1,0:T(8,128)S(1)} fusion(f32[512,1024]{1,0:T(8,128)S(1)} %get-tuple-element.201, f32[1024]{0:T(1024)S(1)} %get-tuple-element.202, f32[1024,128]{1,0:T(8,128)S(1)} %get-tuple-element.220, f32[1024]{0:T(1024)S(1)} %get-tuple-element.205, f32[1024]{0:T(1024)S(1)} %get-tuple-element.206, pred[]{:T(512)S(6)} %compare.4, ...), kind=kOutput, calls=%fused_computation.5.clone.1 | convolution fusion | flops 135790592 | bytes 3289093 | tf_op jit(solution)/shard_map/while/body/eval_jaxpr/dot_general | solution.py:24
  13.5 1.3 %fusion.26 = (f32[1024]{0:T(1024)S(1)}, f32[512,1024]{1,0:T(8,128)S(1)}) fusion(bf16[1024,128]{1,0:T(8,128)(2,1)S(1)} %get-tuple-element.232, bf16[8192,128]{1,0:T(8,128)(2,1)} %get-tuple-element.231, s32[]{:T(128)S(6)} %select_n.22), kind=kOutput, calls=%fused_computation.33.clone.1 | convolution fusion | flops 134740992 | bytes 2494468 | tf_op jit(solution)/shard_map/while/body/eval_jaxpr/dot_general | solution.py:17
  14.9 0.3 fusion.27
  15.2 1.8 %fusion.29 = f32[1024,128]{1,0:T(8,128)S(1)} fusion(f32[512,1024]{1,0:T(8,128)S(1)} %get-tuple-element.201, f32[1024]{0:T(1024)S(1)} %get-tuple-element.202, f32[1024,128]{1,0:T(8,128)S(1)} %get-tuple-element.220, f32[1024]{0:T(1024)S(1)} %get-tuple-element.205, f32[1024]{0:T(1024)S(1)} %get-tuple-element.206, pred[]{:T(512)S(6)} %compare.4, ...), kind=kOutput, calls=%fused_computation.5.clone.1 | convolution fusion | flops 135790592 | bytes 3289093 | tf_op jit(solution)/shard_map/while/body/eval_jaxpr/dot_general | solution.py:24
  17.0 1.4 %fusion.26 = (f32[1024]{0:T(1024)S(1)}, f32[512,1024]{1,0:T(8,128)S(1)}) fusion(bf16[1024,128]{1,0:T(8,128)(2,1)S(1)} %get-tuple-element.232, bf16[8192,128]{1,0:T(8,128)(2,1)} %get-tuple-element.231, s32[]{:T(128)S(6)} %select_n.22), kind=kOutput, calls=%fused_computation.33.clone.1 | convolution fusion | flops 134740992 | bytes 2494468 | tf_op jit(solution)/shard_map/while/body/eval_jaxpr/dot_general | solution.py:17
  18.4 0.3 fusion.27
  18.7 1.8 %fusion.29 = f32[1024,128]{1,0:T(8,128)S(1)} fusion(f32[512,1024]{1,0:T(8,128)S(1)} %get-tuple-element.201, f32[1024]{0:T(1024)S(1)} %get-tuple-element.202, f32[1024,128]{1,0:T(8,128)S(1)} %get-tuple-element.220, f32[1024]{0:T(1024)S(1)} %get-tuple-element.205, f32[1024]{0:T(1024)S(1)} %get-tuple-element.206, pred[]{:T(512)S(6)} %compare.4, ...), kind=kOutput, calls=%fused_computation.5.clone.1 | convolution fusion | flops 135790592 | bytes 3289093 | tf_op jit(solution)/shard_map/while/body/eval_jaxpr/dot_general | solution.py:24
  20.5 1.4 %fusion.26 = (f32[1024]{0:T(1024)S(1)}, f32[512,1024]{1,0:T(8,128)S(1)}) fusion(bf16[1024,128]{1,0:T(8,128)(2,1)S(1)} %get-tuple-element.232, bf16[8192,128]{1,0:T(8,128)(2,1)} %get-tuple-element.231, s32[]{:T(128)S(6)} %select_n.22), kind=kOutput, calls=%fused_computation.33.clone.1 | convolution fusion | flops 134740992 | bytes 2494468 | tf_op jit(solution)/shard_map/while/body/eval_jaxpr/dot_general | solution.py:17
  21.9 0.3 fusion.27
  22.2 1.8 %fusion.29 = f32[1024,128]{1,0:T(8,128)S(1)} fusion(f32[512,1024]{1,0:T(8,128)S(1)} %get-tuple-element.201, f32[1024]{0:T(1024)S(1)} %get-tuple-element.202, f32[1024,128]{1,0:T(8,128)S(1)} %get-tuple-element.220, f32[1024]{0:T(1024)S(1)} %get-tuple-element.205, f32[1024]{0:T(1024)S(1)} %get-tuple-element.206, pred[]{:T(512)S(6)} %compare.4, ...), kind=kOutput, calls=%fused_computation.5.clone.1 | convolution fusion | flops 135790592 | bytes 3289093 | tf_op jit(solution)/shard_map/while/body/eval_jaxpr/dot_general | solution.py:24
  24.0 1.4 %fusion.26 = (f32[1024]{0:T(1024)S(1)}, f32[512,1024]{1,0:T(8,128)S(1)}) fusion(bf16[1024,128]{1,0:T(8,128)(2,1)S(1)} %get-tuple-element.232, bf16[8192,128]{1,0:T(8,128)(2,1)} %get-tuple-element.231, s32[]{:T(128)S(6)} %select_n.22), kind=kOutput, calls=%fused_computation.33.clone.1 | convolution fusion | flops 134740992 | bytes 2494468 | tf_op jit(solution)/shard_map/while/body/eval_jaxpr/dot_general | solution.py:17
  25.4 0.3 fusion.27
  25.7 1.8 %fusion.29 = f32[1024,128]{1,0:T(8,128)S(1)} fusion(f32[512,1024]{1,0:T(8,128)S(1)} %get-tuple-element.201, f32[1024]{0:T(1024)S(1)} %get-tuple-element.202, f32[1024,128]{1,0:T(8,128)S(1)} %get-tuple-element.220, f32[1024]{0:T(1024)S(1)} %get-tuple-element.205, f32[1024]{0:T(1024)S(1)} %get-tuple-element.206, pred[]{:T(512)S(6)} %compare.4, ...), kind=kOutput, calls=%fused_computation.5.clone.1 | convolution fusion | flops 135790592 | bytes 3289093 | tf_op jit(solution)/shard_map/while/body/eval_jaxpr/dot_general | solution.py:24
  27.5 1.4 %fusion.26 = (f32[1024]{0:T(1024)S(1)}, f32[512,1024]{1,0:T(8,128)S(1)}) fusion(bf16[1024,128]{1,0:T(8,128)(2,1)S(1)} %get-tuple-element.232, bf16[8192,128]{1,0:T(8,128)(2,1)} %get-tuple-element.231, s32[]{:T(128)S(6)} %select_n.22), kind=kOutput, calls=%fused_computation.33.clone.1 | convolution fusion | flops 134740992 | bytes 2494468 | tf_op jit(solution)/shard_map/while/body/eval_jaxpr/dot_general | solution.py:17
  28.9 0.3 fusion.27
  29.2 1.8 %fusion.29 = f32[1024,128]{1,0:T(8,128)S(1)} fusion(f32[512,1024]{1,0:T(8,128)S(1)} %get-tuple-element.201, f32[1024]{0:T(1024)S(1)} %get-tuple-element.202, f32[1024,128]{1,0:T(8,128)S(1)} %get-tuple-element.220, f32[1024]{0:T(1024)S(1)} %get-tuple-element.205, f32[1024]{0:T(1024)S(1)} %get-tuple-element.206, pred[]{:T(512)S(6)} %compare.4, ...), kind=kOutput, calls=%fused_computation.5.clone.1 | convolution fusion | flops 135790592 | bytes 3289093 | tf_op jit(solution)/shard_map/while/body/eval_jaxpr/dot_general | solution.py:24
  31.0 1.4 %fusion.26 = (f32[1024]{0:T(1024)S(1)}, f32[512,1024]{1,0:T(8,128)S(1)}) fusion(bf16[1024,128]{1,0:T(8,128)(2,1)S(1)} %get-tuple-element.232, bf16[8192,128]{1,0:T(8,128)(2,1)} %get-tuple-element.231, s32[]{:T(128)S(6)} %select_n.22), kind=kOutput, calls=%fused_computation.33.clone.1 | convolution fusion | flops 134740992 | bytes 2494468 | tf_op jit(solution)/shard_map/while/body/eval_jaxpr/dot_general | solution.py:17
  32.3 0.3 fusion.27
  32.7 1.8 %fusion.29 = f32[1024,128]{1,0:T(8,128)S(1)} fusion(f32[512,1024]{1,0:T(8,128)S(1)} %get-tuple-element.201, f32[1024]{0:T(1024)S(1)} %get-tuple-element.202, f32[1024,128]{1,0:T(8,128)S(1)} %get-tuple-element.220, f32[1024]{0:T(1024)S(1)} %get-tuple-element.205, f32[1024]{0:T(1024)S(1)} %get-tuple-element.206, pred[]{:T(512)S(6)} %compare.4, ...), kind=kOutput, calls=%fused_computation.5.clone.1 | convolution fusion | flops 135790592 | bytes 3289093 | tf_op jit(solution)/shard_map/while/body/eval_jaxpr/dot_general | solution.py:24
  34.5 1.4 %fusion.26 = (f32[1024]{0:T(1024)S(1)}, f32[512,1024]{1,0:T(8,128)S(1)}) fusion(bf16[1024,128]{1,0:T(8,128)(2,1)S(1)} %get-tuple-element.232, bf16[8192,128]{1,0:T(8,128)(2,1)} %get-tuple-element.231, s32[]{:T(128)S(6)} %select_n.22), kind=kOutput, calls=%fused_computation.33.clone.1 | convolution fusion | flops 134740992 | bytes 2494468 | tf_op jit(solution)/shard_map/while/body/eval_jaxpr/dot_general | solution.py:17
  35.8 0.3 fusion.27
  36.2 1.8 %fusion.29 = f32[1024,128]{1,0:T(8,128)S(1)} fusion(f32[512,1024]{1,0:T(8,128)S(1)} %get-tuple-element.201, f32[1024]{0:T(1024)S(1)} %get-tuple-element.202, f32[1024,128]{1,0:T(8,128)S(1)} %get-tuple-element.220, f32[1024]{0:T(1024)S(1)} %get-tuple-element.205, f32[1024]{0:T(1024)S(1)} %get-tuple-element.206, pred[]{:T(512)S(6)} %compare.4, ...), kind=kOutput, calls=%fused_computation.5.clone.1 | convolution fusion | flops 135790592 | bytes 3289093 | tf_op jit(solution)/shard_map/while/body/eval_jaxpr/dot_general | solution.py:24
  38.0 1.4 %fusion.26 = (f32[1024]{0:T(1024)S(1)}, f32[512,1024]{1,0:T(8,128)S(1)}) fusion(bf16[1024,128]{1,0:T(8,128)(2,1)S(1)} %get-tuple-element.232, bf16[8192,128]{1,0:T(8,128)(2,1)} %get-tuple-element.231, s32[]{:T(128)S(6)} %select_n.22), kind=kOutput, calls=%fused_computation.33.clone.1 | convolution fusion | flops 134740992 | bytes 2494468 | tf_op jit(solution)/shard_map/while/body/eval_jaxpr/dot_general | solution.py:17
  39.7 1.8 %fusion.29 = f32[1024,128]{1,0:T(8,128)S(1)} fusion(f32[512,1024]{1,0:T(8,128)S(1)} %get-tuple-element.201, f32[1024]{0:T(1024)S(1)} %get-tuple-element.202, f32[1024,128]{1,0:T(8,128)S(1)} %get-tuple-element.220, f32[1024]{0:T(1024)S(1)} %get-tuple-element.205, f32[1024]{0:T(1024)S(1)} %get-tuple-element.206, pred[]{:T(512)S(6)} %compare.4, ...), kind=kOutput, calls=%fused_computation.5.clone.1 | convolution fusion | flops 135790592 | bytes 3289093 | tf_op jit(solution)/shard_map/while/body/eval_jaxpr/dot_general | solution.py:24
  41.5 1.4 %fusion.26 = (f32[1024]{0:T(1024)S(1)}, f32[512,1024]{1,0:T(8,128)S(1)}) fusion(bf16[1024,128]{1,0:T(8,128)(2,1)S(1)} %get-tuple-element.232, bf16[8192,128]{1,0:T(8,128)(2,1)} %get-tuple-element.231, s32[]{:T(128)S(6)} %select_n.22), kind=kOutput, calls=%fused_computation.33.clone.1 | convolution fusion | flops 134740992 | bytes 2494468 | tf_op jit(solution)/shard_map/while/body/eval_jaxpr/dot_general | solution.py:17
  43.2 1.8 %fusion.29 = f32[1024,128]{1,0:T(8,128)S(1)} fusion(f32[512,1024]{1,0:T(8,128)S(1)} %get-tuple-element.201, f32[1024]{0:T(1024)S(1)} %get-tuple-element.202, f32[1024,128]{1,0:T(8,128)S(1)} %get-tuple-element.220, f32[1024]{0:T(1024)S(1)} %get-tuple-element.205, f32[1024]{0:T(1024)S(1)} %get-tuple-element.206, pred[]{:T(512)S(6)} %compare.4, ...), kind=kOutput, calls=%fused_computation.5.clone.1 | convolution fusion | flops 135790592 | bytes 3289093 | tf_op jit(solution)/shard_map/while/body/eval_jaxpr/dot_general | solution.py:24
  45.0 1.4 %fusion.26 = (f32[1024]{0:T(1024)S(1)}, f32[512,1024]{1,0:T(8,128)S(1)}) fusion(bf16[1024,128]{1,0:T(8,128)(2,1)S(1)} %get-tuple-element.232, bf16[8192,128]{1,0:T(8,128)(2,1)} %get-tuple-element.231, s32[]{:T(128)S(6)} %select_n.22), kind=kOutput, calls=%fused_computation.33.clone.1 | convolution fusion | flops 134740992 | bytes 2494468 | tf_op jit(solution)/shard_map/while/body/eval_jaxpr/dot_general | solution.py:17
  46.3 0.3 fusion.27
  46.7 1.8 %fusion.29 = f32[1024,128]{1,0:T(8,128)S(1)} fusion(f32[512,1024]{1,0:T(8,128)S(1)} %get-tuple-element.201, f32[1024]{0:T(1024)S(1)} %get-tuple-element.202, f32[1024,128]{1,0:T(8,128)S(1)} %get-tuple-element.220, f32[1024]{0:T(1024)S(1)} %get-tuple-element.205, f32[1024]{0:T(1024)S(1)} %get-tuple-element.206, pred[]{:T(512)S(6)} %compare.4, ...), kind=kOutput, calls=%fused_computation.5.clone.1 | convolution fusion | flops 135790592 | bytes 3289093 | tf_op jit(solution)/shard_map/while/body/eval_jaxpr/dot_general | solution.py:24
  48.5 1.4 %fusion.26 = (f32[1024]{0:T(1024)S(1)}, f32[512,1024]{1,0:T(8,128)S(1)}) fusion(bf16[1024,128]{1,0:T(8,128)(2,1)S(1)} %get-tuple-element.232, bf16[8192,128]{1,0:T(8,128)(2,1)} %get-tuple-element.231, s32[]{:T(128)S(6)} %select_n.22), kind=kOutput, calls=%fused_computation.33.clone.1 | convolution fusion | flops 134740992 | bytes 2494468 | tf_op jit(solution)/shard_map/while/body/eval_jaxpr/dot_general | solution.py:17
  50.2 1.8 %fusion.29 = f32[1024,128]{1,0:T(8,128)S(1)} fusion(f32[512,1024]{1,0:T(8,128)S(1)} %get-tuple-element.201, f32[1024]{0:T(1024)S(1)} %get-tuple-element.202, f32[1024,128]{1,0:T(8,128)S(1)} %get-tuple-element.220, f32[1024]{0:T(1024)S(1)} %get-tuple-element.205, f32[1024]{0:T(1024)S(1)} %get-tuple-element.206, pred[]{:T(512)S(6)} %compare.4, ...), kind=kOutput, calls=%fused_computation.5.clone.1 | convolution fusion | flops 135790592 | bytes 3289093 | tf_op jit(solution)/shard_map/while/body/eval_jaxpr/dot_general | solution.py:24
  52.0 1.4 %fusion.26 = (f32[1024]{0:T(1024)S(1)}, f32[512,1024]{1,0:T(8,128)S(1)}) fusion(bf16[1024,128]{1,0:T(8,128)(2,1)S(1)} %get-tuple-element.232, bf16[8192,128]{1,0:T(8,128)(2,1)} %get-tuple-element.231, s32[]{:T(128)S(6)} %select_n.22), kind=kOutput, calls=%fused_computation.33.clone.1 | convolution fusion | flops 134740992 | bytes 2494468 | tf_op jit(solution)/shard_map/while/body/eval_jaxpr/dot_general | solution.py:17
  53.7 1.8 %fusion.29 = f32[1024,128]{1,0:T(8,128)S(1)} fusion(f32[512,1024]{1,0:T(8,128)S(1)} %get-tuple-element.201, f32[1024]{0:T(1024)S(1)} %get-tuple-element.202, f32[1024,128]{1,0:T(8,128)S(1)} %get-tuple-element.220, f32[1024]{0:T(1024)S(1)} %get-tuple-element.205, f32[1024]{0:T(1024)S(1)} %get-tuple-element.206, pred[]{:T(512)S(6)} %compare.4, ...), kind=kOutput, calls=%fused_computation.5.clone.1 | convolution fusion | flops 135790592 | bytes 3289093 | tf_op jit(solution)/shard_map/while/body/eval_jaxpr/dot_general | solution.py:24
  55.4 1.4 %fusion.26 = (f32[1024]{0:T(1024)S(1)}, f32[512,1024]{1,0:T(8,128)S(1)}) fusion(bf16[1024,128]{1,0:T(8,128)(2,1)S(1)} %get-tuple-element.232, bf16[8192,128]{1,0:T(8,128)(2,1)} %get-tuple-element.231, s32[]{:T(128)S(6)} %select_n.22), kind=kOutput, calls=%fused_computation.33.clone.1 | convolution fusion | flops 134740992 | bytes 2494468 | tf_op jit(solution)/shard_map/while/body/eval_jaxpr/dot_general | solution.py:17
  57.2 1.8 %fusion.29 = f32[1024,128]{1,0:T(8,128)S(1)} fusion(f32[512,1024]{1,0:T(8,128)S(1)} %get-tuple-element.201, f32[1024]{0:T(1024)S(1)} %get-tuple-element.202, f32[1024,128]{1,0:T(8,128)S(1)} %get-tuple-element.220, f32[1024]{0:T(1024)S(1)} %get-tuple-element.205, f32[1024]{0:T(1024)S(1)} %get-tuple-element.206, pred[]{:T(512)S(6)} %compare.4, ...), kind=kOutput, calls=%fused_computation.5.clone.1 | convolution fusion | flops 135790592 | bytes 3289093 | tf_op jit(solution)/shard_map/while/body/eval_jaxpr/dot_general | solution.py:24
  58.9 1.4 %fusion.26 = (f32[1024]{0:T(1024)S(1)}, f32[512,1024]{1,0:T(8,128)S(1)}) fusion(bf16[1024,128]{1,0:T(8,128)(2,1)S(1)} %get-tuple-element.232, bf16[8192,128]{1,0:T(8,128)(2,1)} %get-tuple-element.231, s32[]{:T(128)S(6)} %select_n.22), kind=kOutput, calls=%fused_computation.33.clone.1 | convolution fusion | flops 134740992 | bytes 2494468 | tf_op jit(solution)/shard_map/while/body/eval_jaxpr/dot_general | solution.py:17
  60.7 1.8 %fusion.29 = f32[1024,128]{1,0:T(8,128)S(1)} fusion(f32[512,1024]{1,0:T(8,128)S(1)} %get-tuple-element.201, f32[1024]{0:T(1024)S(1)} %get-tuple-element.202, f32[1024,128]{1,0:T(8,128)S(1)} %get-tuple-element.220, f32[1024]{0:T(1024)S(1)} %get-tuple-element.205, f32[1024]{0:T(1024)S(1)} %get-tuple-element.206, pred[]{:T(512)S(6)} %compare.4, ...), kind=kOutput, calls=%fused_computation.5.clone.1 | convolution fusion | flops 135790592 | bytes 3289093 | tf_op jit(solution)/shard_map/while/body/eval_jaxpr/dot_general | solution.py:24
  62.8 26.2 %all_to_all.5 = f32[32,33,128]{2,1,0:T(8,128)S(1)} all-to-all(f32[32,33,128]{2,1,0:T(8,128)S(1)} %pad_maximum_fusion), channel_id=1, replica_groups=mesh['gx'=4,'gy'=8] {'gx','gy'}, dimensions={0} | all-to-all | bytes 1081344 | tf_op jit(solution)/shard_map/all_to_all | solution.py:54
  89.1 0.5 add_subtract_fusion
  89.9 0.7 broadcast_divide_fusion
  (42 shorter events, 3.3 us)
Async XLA Ops:
  0.6 5.8 %copy-start.1 = (s32[1024]{0:T(1024)S(1)}, s32[1024]{0:T(1024)}, u32[]{:S(2)}) copy-start(s32[1024]{0:T(1024)} %param.7) | copy-start | bytes 12292
  0.6 5.5 %copy-start = (bf16[1024,128]{1,0:T(8,128)(2,1)S(1)}, bf16[1024,128]{1,0:T(8,128)(2,1)}, u32[]{:S(2)}) copy-start(bf16[1024,128]{1,0:T(8,128)(2,1)} %param.5) | copy-start | bytes 786436

commit v2 on v1

v2 whole, which is shorter than its diff:
```python
import jax
import jax.numpy as jnp
from jax import lax
from jax.experimental import pallas as pl
from jax.experimental.pallas import tpu as pltpu
from jax.sharding import PartitionSpec as P

AXES = ("gx", "gy")
POS_TILE = 512
ITEM_TILE = 1024


def tile_of(size, tile):
    while size % tile:
        tile //= 2
    return tile


def softmax_kernel(hidden_ref, table_ref, local_ref, acc_ref, stats_ref, *, item_tile):
    hidden = hidden_ref[...]
    positions, lanes = acc_ref.shape
    wanted = jnp.broadcast_to(local_ref[...], (128, positions)).T
    lane = lax.broadcasted_iota(jnp.int32, (positions, 128), 1)
    wanted = wanted - lane
    picked = jnp.zeros((positions, 128), jnp.float32)
    highest = None
    for first in range(0, table_ref.shape[0], item_tile):
        block = table_ref[first:first + item_tile, :]
        scores = lax.dot_general(
            hidden, block, (((1,), (1,)), ((), ())), preferred_element_type=jnp.float32
        )
        for col in range(0, item_tile, 128):
            picked = jnp.where(wanted == first + col, scores[:, col:col + 128], picked)
        new_max = jnp.max(scores, axis=1, keepdims=True)
        if highest is not None:
            new_max = jnp.maximum(highest, new_max)
        probs = jnp.exp(scores - new_max)
        sums = jnp.sum(probs, axis=1, keepdims=True)
        products = jnp.dot(probs.astype(jnp.bfloat16), block, preferred_element_type=jnp.float32)
        if highest is None:
            totals, weighted = sums, products
        else:
            retain = jnp.exp(highest - new_max)
            totals = totals * retain + sums
            weighted = weighted * retain + products
        highest = new_max
    acc_ref[...] = weighted
    logit = jnp.sum(picked, axis=1, keepdims=True)
    stats = jnp.where(lane == 0, highest, jnp.where(lane == 1, totals, logit))
    stats_ref[...] = stats.T[:8]


def local_softmax(hidden_states, item_table, local_index):
    positions, width = hidden_states.shape
    pos_tile = tile_of(positions, POS_TILE)
    item_tile = tile_of(item_table.shape[0], ITEM_TILE)

    def body(*refs):
        softmax_kernel(*refs, item_tile=item_tile)

    return pl.pallas_call(
        body,
        name="block_softmax",
        grid=(positions // pos_tile,),
        in_specs=[
            pl.BlockSpec((pos_tile, width), lambda i: (i, 0)),
            pl.BlockSpec(item_table.shape, lambda i: (0, 0)),
            pl.BlockSpec((1, pos_tile), lambda i: (0, i)),
        ],
        out_specs=[
            pl.BlockSpec((pos_tile, width), lambda i: (i, 0)),
            pl.BlockSpec((8, pos_tile), lambda i: (0, i)),
        ],
        out_shape=[
            jax.ShapeDtypeStruct((positions, width), jnp.float32),
            jax.ShapeDtypeStruct((8, positions), jnp.float32),
        ],
    )(hidden_states, item_table, local_index[None])


def local(hidden_states, item_table, targets):
    positions, lanes = hidden_states.shape
    device_index = lax.axis_index(AXES)
    local_index = targets - device_index * item_table.shape[0]
    weighted, stats = local_softmax(hidden_states, item_table, local_index)
    devices = lax.axis_size(AXES)
    rows = positions // devices
    stats = stats[:3].reshape(3, devices, rows)
    stats = jnp.transpose(stats, (1, 0, 2)).reshape(devices, 3 * rows)
    extra = -(-3 * rows // lanes)
    stats = jnp.pad(stats, ((0, 0), (0, extra * lanes - 3 * rows)))
    payload = jnp.concatenate(
        [weighted.reshape(devices, rows, lanes), stats.reshape(devices, extra, lanes)], axis=1
    )
    got = lax.all_to_all(payload, AXES, 0, 0, tiled=True)
    parts = got[:, rows:].reshape(devices, extra * lanes)
    part_max = parts[:, :rows]
    max_rows = jnp.max(part_max, axis=0)
    factor = jnp.exp(part_max - max_rows[None])
    total_rows = jnp.sum(parts[:, rows:2 * rows] * factor, axis=0)
    target_rows = jnp.sum(parts[:, 2 * rows:3 * rows], axis=0)
    weighted_rows = jnp.sum(got[:, :rows] * factor[:, :, None], axis=0)
    expected = weighted_rows / total_rows[:, None]
    nll = max_rows + jnp.log(total_rows) - target_rows
    return (expected, nll)


def solution(mesh):
    return jax.shard_map(
        local,
        mesh=mesh,
        in_specs=(P(), P(AXES, None), P()),
        out_specs=(P(AXES, None), P(AXES)),
        check_vma=False,
    )
```

time: 91.3 us -> 48.4 us (0.53)
  matrix products: 49.7 us -> 0 us
  Pallas kernels: 0 us -> 16.4 us
  other arithmetic: 8.2 us -> 3.91 us
  local copies, waits for them, and re-layouts: 5.12 us -> 0.99 us
    dot_general x32 -> x0, matrix products: 49.7 us -> none  [the longest x16 28.1 us: visit_block(): block_acc = jnp.dot(probs_low, block, preferred_element_type=jnp.float32)]
    pallas_call x0 -> x1, Pallas kernels: none -> 16.4 us  [local_softmax(): pl.pallas_call(body, name='block_softmax', grid=(positions // pos_tile,),...]
    reduce_sum x17 -> x0, other arithmetic: 5.6 us -> none  [the longest x16 5.39 us: visit_block(): block_sum = jnp.sum(exponent, axis=1)]
    gather x1 -> x0, local copies, waits for them, and re-layouts: 4.74 us -> none  [local(): target_rows = item_table[jnp.clip(local_index, 0, shard_items - 1)]]
    sub x0 -> x1, other arithmetic: none -> 1.28 us  [local(): local_index = targets - device_index * item_table.shape[0]]
    concatenate x1, other arithmetic: 0.06 us -> 1.1 us  [local(): jnp.concatenate([weighted.reshape(devices, rows, lanes), stats.reshape(de...]
where the time goes in v2:
time: 48.4 us; the launch traced here: 48.1 us
  blocking collectives  26.2 us (54%)
  Pallas kernels  16.4 us (34%)
  other arithmetic  3.91 us (8%)
  local copies, waits for them, and re-layouts  0.99 us (2%)
  between operations  0.66 us (1%)
    all_to_all x1, blocking collectives, local(): got = lax.all_to_all(payload, AXES, 0, 0, tiled=True)  26.2 us
    pallas_call x1, Pallas kernels, local_softmax(): pl.pallas_call(body, name='block_softmax', grid=(positions // pos_tile,),...  16.4 us
    sub x1, other arithmetic, local(): local_index = targets - device_index * item_table.shape[0]  1.28 us
    concatenate x1, other arithmetic, local(): jnp.concatenate([weighted.reshape(devices, rows, lanes), stats.reshape(de...  1.1 us

profile of v2, /device:TPU:0, one launch (start us, length us, event | category | flops | bytes accessed | tf_op | source)
XLA Modules:
  0.0 48.1 jit_solution(4110333332321157264)
XLA Ops:
  0.6 1.3 %broadcast_subtract_fusion = s32[1024]{0:T(1024)} fusion(s32[1024]{0:T(1024)} %param.5, s32[]{:T(128)S(6)} %mul.18), kind=kLoop, calls=%fused_computation.10 | loop fusion | flops 1024 | bytes 8196 | tf_op jit(solution)/shard_map/sub | solution.py:84
  1.9 16.4 %block_softmax.1 = (f32[1024,128]{1,0:T(8,128)}, f32[8,1024]{1,0:T(8,128)}) custom-call(bf16[1024,128]{1,0:T(8,128)(2,1)} %refs_0_.1, bf16[8192,128]{1,0:T(8,128)(2,1)} %refs_1_.1, s32[1,1024]{1,0:T(1,128)} %bitcast.14), custom_call_target="tpu_custom_call" | custom-call | tf_op jit(solution)/shard_map/block_softmax/pallas_call | solution.py:61
  18.3 0.8 %slice.18 = f32[3,1024]{1,0:T(4,128)S(1)} slice(f32[8,1024]{1,0:T(8,128)} %get-tuple-element.5), slice={[0:3], [0:1024]} | slice | bytes 24576 | tf_op jit(solution)/shard_map/slice | solution.py:88
  19.1 0.1 reshape.23
  19.2 0.1 reshape.24
  19.3 1.1 %pad_maximum_fusion = f32[32,33,128]{2,1,0:T(8,128)S(1)} fusion(f32[32,1,128]{2,1,0:T(1,128)S(1)} %bitcast.13, f32[32,32,128]{2,1,0:T(8,128)} %bitcast.9), kind=kLoop, calls=%fused_computation | loop fusion | flops 135168 | bytes 1081344 | tf_op jit(solution)/shard_map/concatenate | solution.py:92
  20.4 26.2 %all_to_all.5 = f32[32,33,128]{2,1,0:T(8,128)S(1)} all-to-all(f32[32,33,128]{2,1,0:T(8,128)S(1)} %pad_maximum_fusion), channel_id=1, replica_groups=mesh['gx'=4,'gy'=8] {'gx','gy'}, dimensions={0} | all-to-all | bytes 1081344 | tf_op jit(solution)/shard_map/all_to_all | solution.py:95
  46.6 0.1 slice_reduce_fusion
  46.7 0.5 %add_subtract_fusion = f32[32]{0:T(128)} fusion(f32[32]{0:T(128)S(1)} %get-tuple-element.6, f32[32]{0:T(128)S(1)} %slice_reduce_fusion.1, f32[32]{0:T(128)S(1)} %get-tuple-element.7), kind=kLoop, calls=%fused_computation.11 | loop fusion | flops 64 | bytes 512 | tf_op jit(solution)/shard_map/sub | solution.py:104
  47.2 0.2 fusion
  47.4 0.7 %broadcast_divide_fusion = f32[32,128]{1,0:T(8,128)} fusion(f32[32,128]{1,0:T(8,128)S(1)} %fusion, f32[32]{0:T(128)S(1)} %get-tuple-element.7), kind=kLoop, calls=%fused_computation.9 | loop fusion | flops 4096 | bytes 32896 | tf_op jit(solution)/shard_map/div | solution.py:103
  (4 shorter events, 0.1 us)

commit v3 on v2

v3 whole, which is shorter than its diff:
```python
import jax
import jax.numpy as jnp
from jax import lax
from jax.experimental import pallas as pl
from jax.experimental.pallas import tpu as pltpu
from jax.sharding import PartitionSpec as P

AXES = ("gx", "gy")
ITEM_TILE = 1024


def tile_of(size, tile):
    while size % tile:
        tile //= 2
    return tile


def softmax_kernel(place_ref, hidden_ref, table_ref, targets_ref, out_ref, *, item_tile):
    groups, _, run, width = hidden_ref.shape
    positions = groups * run
    rows = positions // out_ref.shape[0]
    hidden = hidden_ref[...].reshape(positions, width)
    half = place_ref[0]
    wanted = jnp.concatenate(
        [
            jnp.broadcast_to(
                targets_ref[:, pl.ds(pl.multiple_of((2 * g + half) * run, 128), run)], (128, run)
            ).T
            for g in range(groups)
        ],
        axis=0,
    ) - place_ref[1]
    lane = lax.broadcasted_iota(jnp.int32, (positions, 128), 1)
    wanted = wanted - lane
    picked = jnp.zeros((positions, 128), jnp.float32)
    highest = None
    for first in range(0, table_ref.shape[0], item_tile):
        block = table_ref[first:first + item_tile, :]
        scores = lax.dot_general(
            hidden, block, (((1,), (1,)), ((), ())), preferred_element_type=jnp.float32
        )
        for col in range(0, item_tile, 128):
            picked = jnp.where(wanted == first + col, scores[:, col:col + 128], picked)
        new_max = jnp.max(scores, axis=1, keepdims=True)
        if highest is not None:
            new_max = jnp.maximum(highest, new_max)
        probs = jnp.exp(scores - new_max)
        sums = jnp.sum(probs, axis=1, keepdims=True)
        products = jnp.dot(probs.astype(jnp.bfloat16), block, preferred_element_type=jnp.float32)
        if highest is None:
            totals, weighted = sums, products
        else:
            retain = jnp.exp(highest - new_max)
            totals = totals * retain + sums
            weighted = weighted * retain + products
        highest = new_max
    logit = jnp.sum(picked, axis=1, keepdims=True)
    slot = lane - lax.broadcasted_iota(jnp.int32, (positions, 128), 0) % rows
    stats = jnp.where(slot == 0, highest, 0.0)
    stats = jnp.where(slot == rows, totals, stats)
    stats = jnp.where(slot == 2 * rows, logit, stats)
    out_ref[:, :rows, :] = weighted.reshape(-1, rows, width)
    out_ref[:, rows:, :] = jnp.sum(stats.reshape(-1, rows, 128), axis=1, keepdims=True)


def half_softmax(hidden_states, item_table, targets, half, first_item, pairs, devices):
    positions, width = hidden_states.shape
    rows = positions // devices
    run = positions // (2 * pairs)
    item_tile = tile_of(item_table.shape[0], ITEM_TILE)

    def body(*refs):
        softmax_kernel(*refs, item_tile=item_tile)

    return pl.pallas_call(
        body,
        name="half_softmax",
        grid_spec=pltpu.PrefetchScalarGridSpec(
            num_scalar_prefetch=1,
            grid=(1,),
            in_specs=[
                pl.BlockSpec((pairs, 1, run, width), lambda i, place: (0, place[0], 0, 0)),
                pl.BlockSpec(item_table.shape, lambda i, place: (0, 0)),
                pl.BlockSpec((1, positions), lambda i, place: (0, 0)),
            ],
            out_specs=pl.BlockSpec((devices // 2, rows + 1, width), lambda i, place: (0, 0, 0)),
        ),
        out_shape=jax.ShapeDtypeStruct((devices // 2, rows + 1, width), jnp.float32),
    )(
        jnp.stack([half, first_item]),
        hidden_states.reshape(pairs, 2, run, width),
        item_table,
        targets[None],
    )


def local(hidden_states, item_table, targets):
    outer, inner = lax.axis_size("gx"), lax.axis_size("gy")
    devices, pairs = outer * inner, outer // 2
    rows = hidden_states.shape[0] // devices
    device_index = lax.axis_index(AXES)
    first_item = device_index * item_table.shape[0]
    own = lax.axis_index("gx") % 2

    def run(half):
        return half_softmax(hidden_states, item_table, targets, half, first_item, pairs, devices)

    sent = run(1 - own)
    other = lax.ppermute(sent, "gx", [(i, i ^ 1) for i in range(outer)])
    kept = run(own)
    kept_max, other_max = kept[:, rows, :rows], other[:, rows, :rows]
    pair_max = jnp.maximum(kept_max, other_max)
    kept_factor, other_factor = jnp.exp(kept_max - pair_max), jnp.exp(other_max - pair_max)
    weighted = kept[:, :rows] * kept_factor[:, :, None] + other[:, :rows] * other_factor[:, :, None]
    totals = (
        kept[:, rows, rows:2 * rows] * kept_factor + other[:, rows, rows:2 * rows] * other_factor
    )
    logits = kept[:, rows, 2 * rows:3 * rows] + other[:, rows, 2 * rows:3 * rows]
    stats = jnp.concatenate([pair_max, totals, logits], axis=1)
    stats = jnp.pad(stats, ((0, 0), (0, weighted.shape[2] - 3 * rows)))
    payload = jnp.concatenate([weighted, stats[:, None]], axis=1)
    members = [
        [(2 * p + c) * inner + g for p in range(pairs) for g in range(inner)] for c in range(2)
    ]
    got = lax.all_to_all(payload, AXES, 0, 0, axis_index_groups=members, tiled=True)
    parts = got[:, rows]
    part_max = parts[:, :rows]
    max_rows = jnp.max(part_max, axis=0)
    factor = jnp.exp(part_max - max_rows[None])
    total_rows = jnp.sum(parts[:, rows:2 * rows] * factor, axis=0)
    target_rows = jnp.sum(parts[:, 2 * rows:3 * rows], axis=0)
    weighted_rows = jnp.sum(got[:, :rows] * factor[:, :, None], axis=0)
    expected = weighted_rows / total_rows[:, None]
    nll = max_rows + jnp.log(total_rows) - target_rows
    return (expected, nll)


def solution(mesh):
    return jax.shard_map(
        local,
        mesh=mesh,
        in_specs=(P(), P(AXES, None), P()),
        out_specs=(P(AXES, None), P(AXES)),
        check_vma=False,
    )
```

time: 48.4 us -> 46.3 us (0.957)
  blocking collectives: 26.2 us -> 19.6 us
  Pallas kernels: 16.4 us -> 20.2 us
  other arithmetic: 3.91 us -> 4.97 us
  local copies, waits for them, and re-layouts: 0.99 us -> 0.01 us
  starting transfers between devices: 0 us -> 0.49 us
    all_to_all x1, blocking collectives: 26.2 us -> 19.6 us  [local(): lax.all_to_all(payload, AXES, 0, 0, axis_index_groups=members, tiled=True)]
    pallas_call x1 -> x2, Pallas kernels: 16.4 us -> 20.2 us  [half_softmax(): pl.pallas_call(body, name='half_softmax', grid_spec=pltpu.PrefetchScalarG...]
    sub x1 -> x0, other arithmetic: 1.28 us -> none  [local(): local_index = targets - device_index * item_table.shape[0]]
    another operation x0 -> x2, other arithmetic: none -> 1.17 us  [half_softmax(): jnp.stack([half, first_item])]
    add x0 -> x2, other arithmetic: none -> 1.17 us  [the longest x1 1.15 us: local(): kept[:, :rows] * kept_factor[:, :, None]]
    slice x0 -> x1, other arithmetic: none -> 1.08 us  [local(): kept_max, other_max = (kept[:, rows, :rows], other[:, rows, :rows])]
    concatenate x1 -> x2, other arithmetic: 1.1 us -> 0.1 us  [the longest x1 0.08 us: local(): stats = jnp.concatenate([pair_max, totals, logits], axis=1)]
    slice x2 -> x1, local copies, waits for them, and re-layouts: 0.77 us -> 0.01 us  [local(): parts = got[:, rows]]
  transfers between devices with their start and end apart: 0 -> 1, of which waited for: 0 -> 0; matrix products, arithmetic and copies ran while one was open for 0% -> 1% of each run, Pallas kernels for 0% -> 22%
where the time goes in v3:
time: 46.3 us; the launch traced here: 46 us
  Pallas kernels  20.2 us (44%)
  blocking collectives  19.6 us (42%)
  other arithmetic  4.97 us (11%)
  between operations  0.68 us (1%)
  starting transfers between devices  0.49 us (1%)
    pallas_call x2, Pallas kernels, half_softmax(): pl.pallas_call(body, name='half_softmax', grid_spec=pltpu.PrefetchScalarG...  20.2 us
    all_to_all x1, blocking collectives, local(): lax.all_to_all(payload, AXES, 0, 0, axis_index_groups=members, tiled=True)  19.6 us
    another operation x2, other arithmetic, half_softmax(): jnp.stack([half, first_item])  1.17 us
    add x1, other arithmetic, local(): kept[:, :rows] * kept_factor[:, :, None]  1.15 us
    slice x1, other arithmetic, local(): kept_max, other_max = (kept[:, rows, :rows], other[:, rows, :rows])  1.08 us
  transfers between devices with their start and end apart: 1, of which 0 were waited for; matrix products, arithmetic and copies ran while one was open for 1% of the time, Pallas kernels for 22%

profile of v3, /device:TPU:0, one launch (start us, length us, event | category | flops | bytes accessed | tf_op | source)
XLA Modules:
  0.0 46.0 jit_solution(3433227637834724357)
XLA Ops:
  0.6 0.6 %pad_add_fusion.1.refs_0_ = s32[2]{0:T(128)} fusion(s32[1]{0:T(128)} %bitcast.5, s32[1]{0:T(128)} %bitcast.1), kind=kLoop, calls=%fused_computation.20 | loop fusion | flops 2 | bytes 16 | tf_op jit(solution)/shard_map/stack | solution.py:90
  1.2 10.0 %half_softmax.3 = f32[16,33,128]{2,1,0:T(8,128)} custom-call(s32[2]{0:T(128)} %pad_add_fusion.1.refs_0_, bf16[2,2,256,128]{3,2,1,0:T(8,128)(2,1)} %bitcast.22, bf16[8192,128]{1,0:T(8,128)(2,1)} %refs_2_.3, s32[1,1024]{1,0:T(1,128)} %bitcast.32), custom_call_target="tpu_custom_call" | custom-call | tf_op jit(solution)/shard_map/half_softmax/pallas_call | solution.py:75
  11.2 0.5 %collective-permute-start = (f32[16,33,128]{2,1,0:T(8,128)}, f32[16,33,128]{2,1,0:T(8,128)S(1)}, u32[]{:S(2)}, u32[]{:S(2)}) collective-permute-start(f32[16,33,128]{2,1,0:T(8,128)} %half_softmax.3), channel_id=1, source_target_pairs={{0,8},{8,0},{16,24},{24,16},{1,9},{9,1},{17,25},{25,17},{2,10},{10... | collective-permute-start | bytes 811016 | tf_op jit(solution)/shard_map/ppermute | solution.py:109
  11.7 0.6 %pad_add_fusion.refs_0_ = s32[2]{0:T(128)} fusion(s32[1]{0:T(128)} %bitcast, s32[1]{0:T(128)} %bitcast.1), kind=kLoop, calls=%fused_computation.19 | loop fusion | flops 2 | bytes 16 | tf_op jit(solution)/shard_map/stack | solution.py:90
  12.3 10.2 %half_softmax.2 = f32[16,33,128]{2,1,0:T(8,128)} custom-call(s32[2]{0:T(128)} %pad_add_fusion.refs_0_, bf16[2,2,256,128]{3,2,1,0:T(8,128)(2,1)} %bitcast.23, bf16[8192,128]{1,0:T(8,128)(2,1)} %refs_2_.3, s32[1,1024]{1,0:T(1,128)} %bitcast.33), custom_call_target="tpu_custom_call" | custom-call | tf_op jit(solution)/shard_map/half_softmax/pallas_call | solution.py:75
  22.5 0.0 collective-permute-done
  22.5 1.1 %fusion.3 = (f32[16,1,32]{2,1,0:T(1,128)S(1)}, f32[16,1,32]{2,1,0:T(1,128)S(1)}, f32[16,1,32]{2,1,0:T(1,128)S(1)}, f32[16,1,32]{2,1,0:T(1,128)S(1)}, f32[16,1,32]{2,1,0:T(1,128)S(1)}) fusion(f32[16,33,128]{2,1,0:T(8,128)S(1)} %collective-permute-done, f32[16,33,128]{2,1,0:T(8,128)} %half_softmax.2), kind=kLoop, calls=%fused_computation.22 | loop fusion | flops 512 | bytes 22528 | tf_op jit(solution)/shard_map/slice | solution.py:111
  23.6 0.1 select_maximum_fusion
  23.6 1.2 %fusion.1 = f32[16,32,128]{2,1,0:T(8,128)S(1)} fusion(f32[16,33,128]{2,1,0:T(8,128)S(1)} %collective-permute-done, f32[16,33,128]{2,1,0:T(8,128)} %half_softmax.2, f32[16,32]{1,0:T(8,128)S(1)} %get-tuple-element.7, f32[16,32]{1,0:T(8,128)S(1)} %get-tuple-element.6), kind=kLoop, calls=%fused_computation.4 | loop fusion | flops 196608 | bytes 790528 | tf_op jit(solution)/shard_map/add | solution.py:114
  24.8 19.6 %all_to_all.5 = f32[16,33,128]{2,1,0:T(8,128)S(1)} all-to-all(f32[16,33,128]{2,1,0:T(8,128)S(1)} %pad_maximum_fusion), channel_id=1, replica_groups={{0,1,2,3,4,5,6,7,16,17,18,19,20,21,22,23},{8,9,10,11,12,13,14,15,24,25,..., dimensions={0} | all-to-all | bytes 540672 | tf_op jit(solution)/shard_map/all_to_all | solution.py:125
  44.5 0.1 slice_reduce_fusion
  44.6 0.1 fusion
  44.7 0.7 %broadcast_divide_fusion = f32[32,128]{1,0:T(8,128)} fusion(f32[32,128]{1,0:T(8,128)S(1)} %fusion, f32[32]{0:T(128)S(1)} %get-tuple-element.3), kind=kLoop, calls=%fused_computation.13 | loop fusion | flops 4096 | bytes 32896 | tf_op jit(solution)/shard_map/div | solution.py:133
  45.4 0.5 %add_subtract_fusion = f32[32]{0:T(128)} fusion(f32[32]{0:T(128)S(1)} %get-tuple-element.2, f32[32]{0:T(128)S(1)} %slice_reduce_fusion.1, f32[32]{0:T(128)S(1)} %get-tuple-element.3), kind=kLoop, calls=%fused_computation.21 | loop fusion | flops 64 | bytes 512 | tf_op jit(solution)/shard_map/sub | solution.py:134
  (4 shorter events, 0.1 us)
Async XLA Ops:
  11.2 11.3 %collective-permute-start = (f32[16,33,128]{2,1,0:T(8,128)}, f32[16,33,128]{2,1,0:T(8,128)S(1)}, u32[]{:S(2)}, u32[]{:S(2)}) collective-permute-start(f32[16,33,128]{2,1,0:T(8,128)} %half_softmax.3), channel_id=1, source_target_pairs={{0,8},{8,0},{16,24},{24,16},{1,9},{9,1},{17,25},{25,17},{2,10},{10... | collective-permute-start | bytes 811016 | tf_op jit(solution)/shard_map/ppermute | solution.py:109

commit v4 on v3

--- a/solution.py
+++ b/solution.py
@@ -6,7 +6,7 @@
 from jax.sharding import PartitionSpec as P
 
 AXES = ("gx", "gy")
-ITEM_TILE = 1024
+ITEM_TILE = 2048
 
 
 def tile_of(size, tile):
@@ -15,12 +15,12 @@
     return tile
 
 
-def softmax_kernel(place_ref, hidden_ref, table_ref, targets_ref, out_ref, *, item_tile):
+def softmax_kernel(place_ref, hidden_ref, table_ref, targets_ref, out_ref, *, item_tile, turn):
     groups, _, run, width = hidden_ref.shape
     positions = groups * run
     rows = positions // out_ref.shape[0]
     hidden = hidden_ref[...].reshape(positions, width)
-    half = place_ref[0]
+    half = place_ref[turn]
     wanted = jnp.concatenate(
         [
             jnp.broadcast_to(
@@ -29,7 +29,7 @@
             for g in range(groups)
         ],
         axis=0,
-    ) - place_ref[1]
+    ) - place_ref[2]
     lane = lax.broadcasted_iota(jnp.int32, (positions, 128), 1)
     wanted = wanted - lane
     picked = jnp.zeros((positions, 128), jnp.float32)
@@ -63,14 +63,14 @@
     out_ref[:, rows:, :] = jnp.sum(stats.reshape(-1, rows, 128), axis=1, keepdims=True)
 
 
-def half_softmax(hidden_states, item_table, targets, half, first_item, pairs, devices):
+def half_softmax(hidden_states, item_table, targets, place, turn, pairs, devices):
     positions, width = hidden_states.shape
     rows = positions // devices
     run = positions // (2 * pairs)
     item_tile = tile_of(item_table.shape[0], ITEM_TILE)
 
     def body(*refs):
-        softmax_kernel(*refs, item_tile=item_tile)
+        softmax_kernel(*refs, item_tile=item_tile, turn=turn)
 
     return pl.pallas_call(
         body,
@@ -79,7 +79,7 @@
             num_scalar_prefetch=1,
             grid=(1,),
             in_specs=[
-                pl.BlockSpec((pairs, 1, run, width), lambda i, place: (0, place[0], 0, 0)),
+                pl.BlockSpec((pairs, 1, run, width), lambda i, place: (0, place[turn], 0, 0)),
                 pl.BlockSpec(item_table.shape, lambda i, place: (0, 0)),
                 pl.BlockSpec((1, positions), lambda i, place: (0, 0)),
             ],
@@ -87,7 +87,7 @@
         ),
         out_shape=jax.ShapeDtypeStruct((devices // 2, rows + 1, width), jnp.float32),
     )(
-        jnp.stack([half, first_item]),
+        place,
         hidden_states.reshape(pairs, 2, run, width),
         item_table,
         targets[None],
@@ -102,12 +102,14 @@
     first_item = device_index * item_table.shape[0]
     own = lax.axis_index("gx") % 2
 
-    def run(half):
-        return half_softmax(hidden_states, item_table, targets, half, first_item, pairs, devices)
+    place = jnp.stack([1 - own, own, first_item])
 
-    sent = run(1 - own)
+    def run(turn):
+        return half_softmax(hidden_states, item_table, targets, place, turn, pairs, devices)
+
+    sent = run(0)
     other = lax.ppermute(sent, "gx", [(i, i ^ 1) for i in range(outer)])
-    kept = run(own)
+    kept = run(1)
     kept_max, other_max = kept[:, rows, :rows], other[:, rows, :rows]
     pair_max = jnp.maximum(kept_max, other_max)
     kept_factor, other_factor = jnp.exp(kept_max - pair_max), jnp.exp(other_max - pair_max)

time: 46.3 us -> 44.8 us (0.968)
  Pallas kernels: 20.2 us -> 19.3 us
  other arithmetic: 4.97 us -> 4.4 us
    pallas_call x2, Pallas kernels: 20.2 us -> 19.3 us  [half_softmax(): pl.pallas_call(body, name='half_softmax', grid_spec=pltpu.PrefetchScalarG...]
    another operation x2 -> x1, other arithmetic: 1.17 us -> 0.6 us  [local(): place = jnp.stack([1 - own, own, first_item])]
  transfers between devices with their start and end apart: 1 -> 1, of which waited for: 0 -> 0; matrix products, arithmetic and copies ran while one was open for 1% -> 0% of each run, Pallas kernels for 22% -> 22%
where the time goes in v4:
time: 44.8 us; the launch traced here: 44.5 us
  blocking collectives  19.6 us (44%)
  Pallas kernels  19.3 us (43%)
  other arithmetic  4.4 us (10%)
  between operations  0.68 us (2%)
  starting transfers between devices  0.49 us (1%)
    all_to_all x1, blocking collectives, local(): lax.all_to_all(payload, AXES, 0, 0, axis_index_groups=members, tiled=True)  19.6 us
    pallas_call x2, Pallas kernels, half_softmax(): pl.pallas_call(body, name='half_softmax', grid_spec=pltpu.PrefetchScalarG...  19.3 us
    add x1, other arithmetic, local(): kept[:, :rows] * kept_factor[:, :, None]  1.15 us
    slice x1, other arithmetic, local(): kept_max, other_max = (kept[:, rows, :rows], other[:, rows, :rows])  1.08 us
  transfers between devices with their start and end apart: 1, of which 0 were waited for; matrix products, arithmetic and copies ran while one was open for 0% of the time, Pallas kernels for 22%

profile of v4, /device:TPU:0, one launch (start us, length us, event | category | flops | bytes accessed | tf_op | source)
XLA Modules:
  0.0 44.5 jit_solution(5481853342477604437)
XLA Ops:
  0.6 0.6 %pad_add_fusion.refs_0_ = s32[3]{0:T(128)} fusion(s32[1]{0:T(128)} %bitcast.2, s32[1]{0:T(128)} %bitcast.1, s32[1]{0:T(128)} %bitcast), kind=kLoop, calls=%fused_computation.19 | loop fusion | flops 6 | bytes 24 | tf_op jit(solution)/shard_map/stack | solution.py:105
  1.2 9.6 %half_softmax.3 = f32[16,33,128]{2,1,0:T(8,128)} custom-call(s32[3]{0:T(128)} %pad_add_fusion.refs_0_, bf16[2,2,256,128]{3,2,1,0:T(8,128)(2,1)} %bitcast.22, bf16[8192,128]{1,0:T(8,128)(2,1)} %refs_2_.3, s32[1,1024]{1,0:T(1,128)} %bitcast.32), custom_call_target="tpu_custom_call" | custom-call | tf_op jit(solution)/shard_map/half_softmax/pallas_call | solution.py:75
  10.9 0.5 %collective-permute-start = (f32[16,33,128]{2,1,0:T(8,128)}, f32[16,33,128]{2,1,0:T(8,128)S(1)}, u32[]{:S(2)}, u32[]{:S(2)}) collective-permute-start(f32[16,33,128]{2,1,0:T(8,128)} %half_softmax.3), channel_id=1, source_target_pairs={{0,8},{8,0},{16,24},{24,16},{1,9},{9,1},{17,25},{25,17},{2,10},{10... | collective-permute-start | bytes 811016 | tf_op jit(solution)/shard_map/ppermute | solution.py:111
  11.4 9.6 %half_softmax.2 = f32[16,33,128]{2,1,0:T(8,128)} custom-call(s32[3]{0:T(128)} %pad_add_fusion.refs_0_, bf16[2,2,256,128]{3,2,1,0:T(8,128)(2,1)} %bitcast.23, bf16[8192,128]{1,0:T(8,128)(2,1)} %refs_2_.3, s32[1,1024]{1,0:T(1,128)} %bitcast.33), custom_call_target="tpu_custom_call" | custom-call | tf_op jit(solution)/shard_map/half_softmax/pallas_call | solution.py:75
  21.0 0.0 collective-permute-done
  21.0 1.1 %fusion.3 = (f32[16,1,32]{2,1,0:T(1,128)S(1)}, f32[16,1,32]{2,1,0:T(1,128)S(1)}, f32[16,1,32]{2,1,0:T(1,128)S(1)}, f32[16,1,32]{2,1,0:T(1,128)S(1)}, f32[16,1,32]{2,1,0:T(1,128)S(1)}) fusion(f32[16,33,128]{2,1,0:T(8,128)S(1)} %collective-permute-done, f32[16,33,128]{2,1,0:T(8,128)} %half_softmax.2), kind=kLoop, calls=%fused_computation.21 | loop fusion | flops 512 | bytes 22528 | tf_op jit(solution)/shard_map/slice | solution.py:113
  22.1 0.1 select_maximum_fusion
  22.2 1.2 %fusion.1 = f32[16,32,128]{2,1,0:T(8,128)S(1)} fusion(f32[16,33,128]{2,1,0:T(8,128)S(1)} %collective-permute-done, f32[16,33,128]{2,1,0:T(8,128)} %half_softmax.2, f32[16,32]{1,0:T(8,128)S(1)} %get-tuple-element.7, f32[16,32]{1,0:T(8,128)S(1)} %get-tuple-element.6), kind=kLoop, calls=%fused_computation.4 | loop fusion | flops 196608 | bytes 790528 | tf_op jit(solution)/shard_map/add | solution.py:116
  23.4 19.6 %all_to_all.5 = f32[16,33,128]{2,1,0:T(8,128)S(1)} all-to-all(f32[16,33,128]{2,1,0:T(8,128)S(1)} %pad_maximum_fusion), channel_id=1, replica_groups={{0,1,2,3,4,5,6,7,16,17,18,19,20,21,22,23},{8,9,10,11,12,13,14,15,24,25,..., dimensions={0} | all-to-all | bytes 540672 | tf_op jit(solution)/shard_map/all_to_all | solution.py:127
  43.1 0.1 slice_reduce_fusion
  43.1 0.1 fusion
  43.3 0.7 %broadcast_divide_fusion = f32[32,128]{1,0:T(8,128)} fusion(f32[32,128]{1,0:T(8,128)S(1)} %fusion, f32[32]{0:T(128)S(1)} %get-tuple-element.3), kind=kLoop, calls=%fused_computation.13 | loop fusion | flops 4096 | bytes 32896 | tf_op jit(solution)/shard_map/div | solution.py:135
  44.0 0.5 %add_subtract_fusion = f32[32]{0:T(128)} fusion(f32[32]{0:T(128)S(1)} %get-tuple-element.2, f32[32]{0:T(128)S(1)} %slice_reduce_fusion.1, f32[32]{0:T(128)S(1)} %get-tuple-element.3), kind=kLoop, calls=%fused_computation.20 | loop fusion | flops 64 | bytes 512 | tf_op jit(solution)/shard_map/sub | solution.py:136
  (4 shorter events, 0.1 us)
Async XLA Ops:
  10.9 10.1 %collective-permute-start = (f32[16,33,128]{2,1,0:T(8,128)}, f32[16,33,128]{2,1,0:T(8,128)S(1)}, u32[]{:S(2)}, u32[]{:S(2)}) collective-permute-start(f32[16,33,128]{2,1,0:T(8,128)} %half_softmax.3), channel_id=1, source_target_pairs={{0,8},{8,0},{16,24},{24,16},{1,9},{9,1},{17,25},{25,17},{2,10},{10... | collective-permute-start | bytes 811016 | tf_op jit(solution)/shard_map/ppermute | solution.py:111
